TPU v7x, 32 devices: a whole 2x2x4 slice. The times are simulated.
32 devices in a mesh: grp: 2 (over x), seq: 16 (over z, y, core).
Axes of the slice: x: 2, y: 2, z: 4, core: 2. Of those that a mesh axis runs over, the one named last changes fastest.
Arguments:
- llm_grad: bfloat16 [4096, 8192], P('seq', 'grp'), may hold values from -6 to 6
- image_grid: int32 [256, 2], replicated, may hold values from 1 to 3, as said below
- image_owner: int32 [256], replicated, may hold values from 0 to 15, as said below
- row_start: int32 [256], replicated, may hold values from 0 to 255, as said below
- merger_pre: bfloat16 [48, 16, 2560], P(None, 'seq', 'grp'), may hold values from -6 to 6
- vit_out: bfloat16 [192, 16, 1280], P(None, 'seq'), may hold values from -6 to 6
- vit_pre: bfloat16 [192, 16, 2560], P(None, 'seq', 'grp'), may hold values from -6 to 6
- ln_gain: float32 [1280], replicated, may hold values from 0.25 to 1.75
- merger_out_w: bfloat16 [8192, 2560], P('seq', 'grp'), may hold values from -0.0625 to 0.0625
- merger_in_w: bfloat16 [2560, 5120], P('grp', 'seq'), may hold values from -0.125 to 0.125
- vit_fc2_w: bfloat16 [1280, 2560], P('seq', 'grp'), may hold values from -0.15625 to 0.15625
Outputs:
- patch_grad: bfloat16 [192, 16, 1280], P('grp', 'seq')
- fc1_grad: bfloat16 [192, 16, 2560], P(None, 'seq', 'grp')
- fc2_w_grad: float32 [1280, 2560], P('seq', 'grp')
Inputs may be any that keep to these rules, and one draw needn't show every extreme that they name: `image_grid`: height times width is 1 to 3; the first image of every shard is 1 by 3; the last image of shard 0 is 1 by 1. `image_owner`: the 16 images of one shard have 16 different owners. An image's rows row_start to row_start + t - 1 lie inside its shard and meet no other image's rows; a shard's images follow the order of k; the last image of every shard ends at the shard's last row; the first image of shard 0 starts at row 0.
All inputs are finite; a program needn't handle non-finite values.
Results may differ from a plain program's by a relative error of at most 0.02.
Values may be sent and summed in bfloat16 or wider, within the bound.
A program may use at most 128 MiB of HBM per device.

v0:
```python
import jax
import jax.numpy as jnp
from jax import lax
from jax.sharding import PartitionSpec as P

SLOT = 3


def gelu_slope(values):
    return (
        0.5 * (1.0 + lax.erf(values * 0.7071067811865476))
        + values * jnp.exp(-0.5 * values * values) * 0.3989422804014327
    )


def patch_table(widths, counts, slots):
    places = jnp.arange(4 * slots, dtype=jnp.int32)
    merged = places // 4
    corner = places % 4
    row_in = merged[None, :] // widths[:, None]
    col_in = merged[None, :] % widths[:, None]
    target = (
        (2 * row_in + corner[None, :] // 2) * (2 * widths[:, None])
        + 2 * col_in
        + corner[None, :] % 2
    )
    usable = merged[None, :] < counts[:, None]
    return ((target[:, None, :] == places[None, :, None]) & usable[:, None, :]).astype(jnp.float32)


def norm_backward(upstream, inputs, scales):
    average = jnp.mean(inputs, -1, keepdims=True)
    centred = inputs - average
    inverse_std = lax.rsqrt(jnp.mean(centred * centred, -1, keepdims=True) + 1e-06)
    normed = centred * inverse_std
    scaled = upstream * scales
    return inverse_std * (
        scaled
        - jnp.mean(scaled, -1, keepdims=True)
        - normed * jnp.mean(scaled * normed, -1, keepdims=True)
    )


def on_device(
    llm_grad,
    image_grid,
    image_owner,
    row_start,
    merger_pre,
    vit_out,
    vit_pre,
    ln_gain,
    merger_out_w,
    merger_in_w,
    vit_fc2_w,
):
    seq_count = lax.axis_size("seq")
    own_index = lax.axis_index("seq")
    grids = image_grid.reshape(seq_count, seq_count, 2)
    counts = grids[:, :, 0] * grids[:, :, 1]
    widths = grids[:, :, 1]
    owners = image_owner.reshape(seq_count, seq_count)
    starts = row_start.reshape(seq_count, seq_count)
    within = jnp.arange(SLOT, dtype=jnp.int32)
    peers = jnp.arange(seq_count, dtype=jnp.int32)
    shard_rows = llm_grad.shape[0]
    my_owners = lax.dynamic_index_in_dim(owners, own_index, 0, keepdims=False)
    my_counts = lax.dynamic_index_in_dim(counts, own_index, 0, keepdims=False)
    my_starts = lax.dynamic_index_in_dim(starts, own_index, 0, keepdims=False)
    targets = (my_owners[None, :] == peers[:, None]).astype(jnp.int32)
    send_counts = jnp.sum(targets * my_counts[None, :], 1)
    send_starts = jnp.sum(targets * my_starts[None, :], 1)
    indices = jnp.minimum(send_starts[:, None] + within[None, :], shard_rows - 1)
    usable = within[None, :] < send_counts[:, None]
    picked = jnp.take(llm_grad, indices.reshape(-1), axis=0)
    outgoing = jnp.where(usable.reshape(-1, 1), picked, jnp.zeros_like(picked)).reshape(
        seq_count, SLOT, llm_grad.shape[1]
    )
    received = (owners == own_index).astype(jnp.int32)
    recv_counts = jnp.sum(received * counts, 1)
    recv_widths = jnp.sum(received * widths, 1)
    wide_rows = lax.all_gather(outgoing, "grp", axis=2, tiled=True)
    flat = wide_rows.reshape(-1, wide_rows.shape[2])
    columns = flat
    folded = jnp.dot(
        columns,
        lax.all_gather(merger_out_w, "seq", axis=0, tiled=True),
        preferred_element_type=jnp.float32,
    )
    source_grad = folded.astype(jnp.bfloat16).reshape(seq_count, SLOT, merger_out_w.shape[1])
    arrived = lax.all_to_all(source_grad, "seq", split_axis=0, concat_axis=0, tiled=True)
    unit_grad = arrived.reshape(seq_count * SLOT, merger_out_w.shape[1])
    pre_act = merger_pre[:, 0, :].astype(jnp.float32)
    pre_grad = (gelu_slope(pre_act) * unit_grad.astype(jnp.float32)).astype(jnp.bfloat16)
    merged_part = jnp.dot(
        pre_grad,
        lax.all_gather(merger_in_w, "seq", axis=1, tiled=True),
        preferred_element_type=jnp.float32,
    )
    vit_width = vit_out.shape[2]
    table = patch_table(recv_widths, recv_counts, SLOT)
    patch_part = jnp.einsum(
        "spq,sqc->spc",
        table,
        merged_part.reshape(seq_count, 4 * SLOT, vit_width),
        precision=lax.Precision.HIGHEST,
    ).reshape(-1, vit_width)
    patch_in = lax.psum(patch_part.astype(jnp.bfloat16), "grp").astype(jnp.float32)
    patch_grad = norm_backward(patch_in, vit_out[:, 0, :].astype(jnp.float32), ln_gain).astype(
        jnp.bfloat16
    )
    group_rows = patch_grad.shape[0] // lax.axis_size("grp")
    own_rows = lax.dynamic_slice_in_dim(
        patch_grad, lax.axis_index("grp") * group_rows, group_rows, 0
    )
    columns = patch_grad
    act_grad = jnp.dot(
        columns,
        lax.all_gather(vit_fc2_w, "seq", axis=0, tiled=True),
        preferred_element_type=jnp.float32,
    )
    fc_in = vit_pre[:, 0, :].astype(jnp.float32)
    sigmoid_q = jax.nn.sigmoid(1.702 * fc_in)
    activation = (fc_in * sigmoid_q).astype(jnp.bfloat16)
    fc1_grad = ((sigmoid_q + 1.702 * fc_in * sigmoid_q * (1.0 - sigmoid_q)) * act_grad).astype(
        jnp.bfloat16
    )
    columns = patch_grad
    weight_grad = lax.psum_scatter(
        lax.dot_general(
            columns, activation, (((0,), (0,)), ((), ())), preferred_element_type=jnp.float32
        ),
        "seq",
        scatter_dimension=0,
        tiled=True,
    )
    return (
        own_rows.reshape(group_rows, 1, vit_width),
        fc1_grad.reshape(-1, 1, vit_pre.shape[2]),
        weight_grad,
    )


def solution(mesh):
    return jax.shard_map(
        on_device,
        mesh=mesh,
        in_specs=(
            P("seq", "grp"),
            P(),
            P(),
            P(),
            P(None, "seq", "grp"),
            P(None, "seq", None),
            P(None, "seq", "grp"),
            P(),
            P("seq", "grp"),
            P("grp", "seq"),
            P("seq", "grp"),
        ),
        out_specs=(P("grp", "seq", None), P(None, "seq", "grp"), P("seq", "grp")),
        check_vma=False,
    )
```

profile of v0, /device:TPU:13, one launch (start us, length us, event | category | flops | bytes accessed | tf_op | source)
XLA Modules:
  0.0 413.9 jit_solution(1489986869144480326)
XLA Ops:
  7.2 0.7 all-gather.4.cloned.1.call-update
  8.0 0.7 all-gather.6.cloned.1.call-update
  8.7 0.8 reshape.409
  9.4 0.8 reshape.410
  10.2 0.8 reshape.411
  11.4 0.8 gather_fusion
  12.2 0.2 gather.7
  12.6 0.4 select_select_fusion
  13.0 13.6 %all_gather.12 = bf16[16,3,8192]{2,1,0:T(4,128)(2,1)} all-gather(bf16[16,3,4096]{2,1,0:T(4,128)(2,1)S(1)} %select_select_fusion), channel_id=1, replica_groups=mesh['grp'=2,'seq'=16] {'grp'}, dimensions={2}, use_global_device_ids=true | all-gather | bytes 1179648 | tf_op jit(solution)/shard_map/all_gather | solution.py:82
  26.6 1.8 reshape.412
  28.5 91.2 %all-gather.4.cloned.1.call-done = bf16[8192,1280]{1,0:T(8,128)(2,1)} async-done(((bf16[512,1280]{1,0:T(8,128)(2,1)}), bf16[8192,1280]{1,0:T(8,128)(2,1)}) %all-gather.4.cloned.1.call-update) | async-done | bytes 20971536 | tf_op jit(solution)/shard_map/all_gather | solution.py:87
  119.7 8.9 %convolution_convert_fusion.1 = bf16[48,1280]{1,0:T(8,128)(2,1)S(1)} fusion(bf16[48,8192]{1,0:T(8,128)(2,1)S(1)} %reshape.412, bf16[8192,1280]{1,0:T(8,128)(2,1)} %all-gather.4.cloned.1.call-done), kind=kOutput, calls=%fused_computation.5 | convolution fusion | flops 1006694400 | bytes 21880832 | tf_op jit(solution)/shard_map/dot_general | solution.py:85
  128.6 0.7 reshape.413
  129.3 5.2 %all-to-all-start = ((bf16[16,3,1280]{2,1,0:T(4,128)(2,1)}), bf16[16,3,1280]{2,1,0:T(4,128)(2,1)S(1)}, u32[]{:S(2)}, u32[]{:S(2)}) async-start(bf16[16,3,1280]{2,1,0:T(4,128)(2,1)} %reshape.413), calls=%async_computation | async-start | bytes 327680 | tf_op jit(solution)/shard_map/all_to_all | solution.py:91
  134.6 0.3 fusion.50
  134.8 10.4 %all-to-all-done = bf16[16,3,1280]{2,1,0:T(4,128)(2,1)S(1)} async-done(((bf16[16,3,1280]{2,1,0:T(4,128)(2,1)}), bf16[16,3,1280]{2,1,0:T(4,128)(2,1)S(1)}, u32[]{:S(2)}, u32[]{:S(2)}) %all-to-all-start) | async-done | bytes 122912 | tf_op jit(solution)/shard_map/all_to_all | solution.py:91
  145.3 82.1 %all-gather.6.cloned.1.call-done = bf16[1280,5120]{0,1:T(8,128)(2,1)} async-done(((bf16[1280,320]{0,1:T(8,128)(2,1)}), bf16[1280,5120]{0,1:T(8,128)(2,1)}) %all-gather.6.cloned.1.call-update) | async-done | bytes 13107216 | tf_op jit(solution)/shard_map/all_gather | solution.py:97
  227.3 9.6 %fusion.36 = f32[48,5120]{1,0:T(8,128)} fusion(bf16[1280,5120]{0,1:T(8,128)(2,1)} %all-gather.6.cloned.1.call-done, f32[48,1280]{1,0:T(8,128)S(1)} %reshape.418, bf16[48,1,1280]{2,0,1:T(8,128)(2,1)S(1)} %copy-done.3), kind=kOutput, calls=%fused_computation.50 | convolution fusion | flops 629821440 | bytes 14458880 | tf_op jit(solution)/shard_map/dot_general | solution.py:95
  237.0 2.6 reshape.414
  239.6 2.1 convolution_convert_fusion
  241.6 0.9 convert_element_type.60
  242.6 0.5 all-gather.8.cloned.1.call-update
  243.2 0.1 convert_reduce_fusion
  243.3 0.3 fusion.18
  243.6 26.7 %all-reduce.2.cloned.1.call-done = bf16[192,1280]{1,0:T(8,128)(2,1)} async-done(((bf16[192,1280]{1,0:T(8,128)(2,1)}), bf16[192,1280]{1,0:T(8,128)(2,1)}) %all-reduce.2.cloned.1.call-update) | async-done | bytes 491536 | tf_op jit(solution)/shard_map/psum | solution.py:108
  270.4 1.4 fusion.20
  271.8 1.4 fusion.17
  273.2 4.8 %fusion.21 = f32[1280,1280]{1,0:T(8,128)} fusion(bf16[192,1280]{1,0:T(8,128)(2,1)S(1)} %fusion.17, bf16[192,1,1280]{2,0,1:T(8,128)(2,1)} %param.17), kind=kOutput, calls=%fused_computation.31 | convolution fusion | flops 630865920 | bytes 7536640 | tf_op jit(solution)/shard_map/dot_general | solution.py:130
  278.0 0.7 dynamic-slice_bitcast_fusion
  278.8 39.5 %all-gather.8.cloned.1.call-done = bf16[1280,1280]{1,0:T(8,128)(2,1)} async-done(((bf16[80,1280]{1,0:T(8,128)(2,1)}), bf16[1280,1280]{1,0:T(8,128)(2,1)}) %all-gather.8.cloned.1.call-update) | async-done | bytes 3276816 | tf_op jit(solution)/shard_map/all_gather | solution.py:119
  318.2 3.6 fusion.1
  321.8 85.5 %reduce-scatter.2.cloned.1.call-done = f32[80,1280]{1,0:T(8,128)} async-done(((f32[1280,1280]{1,0:T(8,128)}), f32[80,1280]{1,0:T(8,128)}) %reduce-scatter.2.cloned.1.call-update) | async-done | bytes 409616 | tf_op jit(solution)/shard_map/reduce_scatter | solution.py:129
  (37 shorter events, 1.0 us)
Async XLA Ops:
  7.2 4.2 %copy-start = (bf16[256,4096]{1,0:T(8,128)(2,1)S(1)}, bf16[256,4096]{1,0:T(8,128)(2,1)}, u32[]{:S(2)}) copy-start(bf16[256,4096]{1,0:T(8,128)(2,1)} %param.11) | copy-start | bytes 6291460
  7.2 112.5 %all-gather.4.cloned.1.call-start = ((), (), s32[]{:S(2)}) async-start(), calls=%async_computation.2 | async-start | bytes 22282240 | tf_op jit(solution)/shard_map/all_gather | solution.py:87
  7.9 219.4 %all-gather.6.cloned.1.call-start = ((), (), s32[]{:S(2)}) async-start(), calls=%async_computation.3 | async-start | bytes 13926400 | tf_op jit(solution)/shard_map/all_gather | solution.py:97
  28.5 198.8 %copy-start.3 = (bf16[48,1,1280]{2,0,1:T(8,128)(2,1)S(1)}, bf16[48,1,1280]{2,0,1:T(8,128)(2,1)}, u32[]{:S(2)}) copy-start(bf16[48,1,1280]{2,0,1:T(8,128)(2,1)} %param.15) | copy-start | bytes 368644
  129.3 15.9 %all-to-all-start = ((bf16[16,3,1280]{2,1,0:T(4,128)(2,1)}), bf16[16,3,1280]{2,1,0:T(4,128)(2,1)S(1)}, u32[]{:S(2)}, u32[]{:S(2)}) async-start(bf16[16,3,1280]{2,1,0:T(4,128)(2,1)} %reshape.413), calls=%async_computation | async-start | bytes 327680 | tf_op jit(solution)/shard_map/all_to_all | solution.py:91
  134.5 135.8 %all-reduce.2.cloned.1.call-start = ((), (), s32[]{:S(2)}) async-start(), calls=%async_computation.4 | async-start | bytes 983040 | tf_op jit(solution)/shard_map/psum | solution.py:108
  237.0 6.2 %copy-start.1 = (bf16[192,1,1280]{2,0,1:T(8,128)(2,1)S(1)}, bf16[192,1,1280]{2,0,1:T(8,128)(2,1)}, u32[]{:S(2)}) copy-start(bf16[192,1,1280]{2,0,1:T(8,128)(2,1)} %param.16) | copy-start | bytes 1474564
  237.0 33.4 %copy-start.4 = (f32[1280]{0:T(1024)S(1)}, f32[1280]{0:T(1024)}, u32[]{:S(2)}) copy-start(f32[1280]{0:T(1024)} %param.18) | copy-start | bytes 15364
  242.5 75.7 %all-gather.8.cloned.1.call-start = ((), (), s32[]{:S(2)}) async-start(), calls=%async_computation.5 | async-start | bytes 3481600 | tf_op jit(solution)/shard_map/all_gather | solution.py:119
  243.1 164.2 %reduce-scatter.2.cloned.1.call-start = ((), (), s32[]{:S(2)}) async-start(), calls=%async_computation.6 | async-start | bytes 6963200 | tf_op jit(solution)/shard_map/reduce_scatter | solution.py:129
  278.0 40.2 %copy-start.2 = (bf16[192,1,1280]{2,0,1:T(8,128)(2,1)S(1)}, bf16[192,1,1280]{2,0,1:T(8,128)(2,1)}, u32[]{:S(2)}) copy-start(bf16[192,1,1280]{2,0,1:T(8,128)(2,1)} %param.17) | copy-start | bytes 1474564
Sparse Core Ops, SparseCore 0:
  9.6 110.0 all-gather.3
  122.0 105.3 all-gather.5
  242.7 27.6 all-reduce.1
  272.5 45.6 all-gather.7
  322.6 84.6 reduce-scatter.1
where the time goes:
time: 417 us; the launch traced here: 414 us
  waiting for transfers between devices  337 us (81%)
  matrix products  29 us (7%)
  between operations  14 us (3%)
  blocking collectives  13.6 us (3%)
  local copies, waits for them, and re-layouts  10.2 us (2%)
  starting transfers between devices  5.42 us (1%)
  other arithmetic  4.46 us (1%)
    all_gather x1, waiting for transfers between devices, on_device(): lax.all_gather(merger_out_w, 'seq', axis=0, tiled=True)  91.2 us
    reduce_scatter x1, waiting for transfers between devices, on_device(): lax.psum_scatter(lax.dot_general(columns, activation, (((0,), (0,)), ((),...  85.5 us
    all_gather x1, waiting for transfers between devices, on_device(): lax.all_gather(merger_in_w, 'seq', axis=1, tiled=True)  82.1 us
    all_gather x1, waiting for transfers between devices, on_device(): lax.all_gather(vit_fc2_w, 'seq', axis=0, tiled=True)  39.5 us
    psum x1, waiting for transfers between devices, on_device(): lax.psum(patch_part.astype(jnp.bfloat16), 'grp').astype(jnp.float32)  26.7 us
    all_gather x1, blocking collectives, on_device(): wide_rows = lax.all_gather(outgoing, 'grp', axis=2, tiled=True)  13.6 us
    all_to_all x1, waiting for transfers between devices, on_device(): lax.all_to_all(source_grad, 'seq', split_axis=0, concat_axis=0, tiled=True)  10.4 us
    dot_general x1, matrix products, on_device(): jnp.dot(pre_grad, lax.all_gather(merger_in_w, 'seq', axis=1, tiled=True),...  9.61 us
  transfers between devices with their start and end apart: 6, of which 6 were waited for; matrix products, arithmetic and copies ran while one was open for 7% of the time, Pallas kernels for 0%

commit v1 on v0

--- a/solution.py
+++ b/solution.py
@@ -79,33 +79,39 @@
     received = (owners == own_index).astype(jnp.int32)
     recv_counts = jnp.sum(received * counts, 1)
     recv_widths = jnp.sum(received * widths, 1)
-    wide_rows = lax.all_gather(outgoing, "grp", axis=2, tiled=True)
-    flat = wide_rows.reshape(-1, wide_rows.shape[2])
-    columns = flat
-    folded = jnp.dot(
-        columns,
-        lax.all_gather(merger_out_w, "seq", axis=0, tiled=True),
-        preferred_element_type=jnp.float32,
+    wide_rows = lax.all_gather(
+        outgoing.reshape(-1, llm_grad.shape[1]), "grp", axis=1, tiled=True
     )
-    source_grad = folded.astype(jnp.bfloat16).reshape(seq_count, SLOT, merger_out_w.shape[1])
-    arrived = lax.all_to_all(source_grad, "seq", split_axis=0, concat_axis=0, tiled=True)
-    unit_grad = arrived.reshape(seq_count * SLOT, merger_out_w.shape[1])
+    sliced = lax.all_to_all(wide_rows, "seq", split_axis=1, concat_axis=0, tiled=True)
+    features = sliced.shape[1]
+    by_owner = jnp.swapaxes(
+        sliced.reshape(seq_count, seq_count, SLOT, features), 0, 1
+    ).reshape(-1, features)
+    folded = jnp.dot(by_owner, merger_out_w, preferred_element_type=jnp.float32)
+    arrived = lax.all_to_all(
+        folded.astype(jnp.bfloat16), "seq", split_axis=0, concat_axis=0, tiled=True
+    )
+    unit_grad = jnp.sum(
+        arrived.reshape(seq_count, seq_count * SLOT, -1).astype(jnp.float32), 0
+    ).astype(jnp.bfloat16)
     pre_act = merger_pre[:, 0, :].astype(jnp.float32)
     pre_grad = (gelu_slope(pre_act) * unit_grad.astype(jnp.float32)).astype(jnp.bfloat16)
-    merged_part = jnp.dot(
-        pre_grad,
-        lax.all_gather(merger_in_w, "seq", axis=1, tiled=True),
-        preferred_element_type=jnp.float32,
+    all_pre = lax.all_gather(pre_grad, "seq", axis=0, tiled=True)
+    part_cols = jnp.dot(all_pre, merger_in_w, preferred_element_type=jnp.float32)
+    part_rows = lax.all_to_all(
+        part_cols.astype(jnp.bfloat16), "seq", split_axis=0, concat_axis=1, tiled=True
+    )
+    merged_part = jnp.sum(
+        lax.all_gather(part_rows, "grp", axis=0).astype(jnp.float32), 0
     )
     vit_width = vit_out.shape[2]
     table = patch_table(recv_widths, recv_counts, SLOT)
-    patch_part = jnp.einsum(
+    patch_in = jnp.einsum(
         "spq,sqc->spc",
         table,
         merged_part.reshape(seq_count, 4 * SLOT, vit_width),
         precision=lax.Precision.HIGHEST,
     ).reshape(-1, vit_width)
-    patch_in = lax.psum(patch_part.astype(jnp.bfloat16), "grp").astype(jnp.float32)
     patch_grad = norm_backward(patch_in, vit_out[:, 0, :].astype(jnp.float32), ln_gain).astype(
         jnp.bfloat16
     )
@@ -126,13 +132,14 @@
         jnp.bfloat16
     )
     columns = patch_grad
-    weight_grad = lax.psum_scatter(
-        lax.dot_general(
-            columns, activation, (((0,), (0,)), ((), ())), preferred_element_type=jnp.float32
-        ),
-        "seq",
-        scatter_dimension=0,
-        tiled=True,
+    weight_part = lax.dot_general(
+        columns, activation, (((0,), (0,)), ((), ())), preferred_element_type=jnp.float32
+    )
+    weight_parts = lax.all_to_all(
+        weight_part.astype(jnp.bfloat16), "seq", split_axis=0, concat_axis=0, tiled=True
+    )
+    weight_grad = jnp.sum(
+        weight_parts.reshape(seq_count, -1, weight_part.shape[1]).astype(jnp.float32), 0
     )
     return (
         own_rows.reshape(group_rows, 1, vit_width),

time: 417 us -> 298 us (0.71)
  waiting for transfers between devices: 337 us -> 124 us
  blocking collectives: 13.6 us -> 99.9 us
  matrix products: 29 us -> 15.2 us
  local copies, waits for them, and re-layouts: 10.2 us -> 19.6 us
  other arithmetic: 4.46 us -> 11.3 us
  starting transfers between devices: 5.42 us -> 12.2 us
    all_gather x2 -> x1, waiting for transfers between devices: 173 us -> 38 us  [on_device(): all_pre = lax.all_gather(pre_grad, 'seq', axis=0, tiled=True)]
    reduce_scatter x1 -> x0, waiting for transfers between devices: 85.5 us -> none  [on_device(): lax.psum_scatter(lax.dot_general(columns, activation, (((0,), (0,)), ((),...]
    all_to_all x0 -> x2, blocking collectives: none -> 75.6 us  [the longest x1 49.2 us: on_device(): lax.all_to_all(folded.astype(jnp.bfloat16), 'seq', split_axis=0, concat_a...]
    all_to_all x1 -> x2, waiting for transfers between devices: 10.4 us -> 85.6 us  [the longest x1 65.5 us: on_device(): lax.all_to_all(weight_part.astype(jnp.bfloat16), 'seq', split_axis=0, con...]
    all_gather x1, waiting for transfers between devices: 39.5 us -> 0.01 us  [on_device(): lax.all_gather(vit_fc2_w, 'seq', axis=0, tiled=True)]
    psum x1 -> x0, waiting for transfers between devices: 26.7 us -> none  [on_device(): lax.psum(patch_part.astype(jnp.bfloat16), 'grp').astype(jnp.float32)]
    dot_general x2, matrix products: 18.5 us -> 5.31 us  [the longest x1 2.74 us: on_device(): folded = jnp.dot(by_owner, merger_out_w, preferred_element_type=jnp.float32)]
    all_gather x1 -> x2, blocking collectives: 13.6 us -> 24.3 us  [the longest x1 13.6 us: on_device(): lax.all_gather(part_rows, 'grp', axis=0).astype(jnp.float32)]
  transfers between devices with their start and end apart: 6 -> 4, of which waited for: 6 -> 3; matrix products, arithmetic and copies ran while one was open for 7% -> 9% of each run, Pallas kernels for 0% -> 0%
where the time goes in v1:
time: 298 us; the launch traced here: 297 us
  waiting for transfers between devices  124 us (42%)
  blocking collectives  99.9 us (34%)
  local copies, waits for them, and re-layouts  19.6 us (7%)
  matrix products  15.2 us (5%)
  between operations  14.3 us (5%)
  starting transfers between devices  12.2 us (4%)
  other arithmetic  11.3 us (4%)
    all_to_all x1, waiting for transfers between devices, on_device(): lax.all_to_all(weight_part.astype(jnp.bfloat16), 'seq', split_axis=0, con...  65.5 us
    all_to_all x1, blocking collectives, on_device(): lax.all_to_all(folded.astype(jnp.bfloat16), 'seq', split_axis=0, concat_a...  49.2 us
    all_gather x1, waiting for transfers between devices, on_device(): all_pre = lax.all_gather(pre_grad, 'seq', axis=0, tiled=True)  38 us
    all_to_all x1, blocking collectives, on_device(): lax.all_to_all(wide_rows, 'seq', split_axis=1, concat_axis=0, tiled=True)  26.4 us
    all_to_all x1, waiting for transfers between devices, on_device(): lax.all_to_all(part_cols.astype(jnp.bfloat16), 'seq', split_axis=0, conca...  20.1 us
    all_gather x1, blocking collectives, on_device(): lax.all_gather(part_rows, 'grp', axis=0).astype(jnp.float32)  13.6 us
    all_gather x1, blocking collectives, on_device(): lax.all_gather(outgoing.reshape(-1, llm_grad.shape[1]), 'grp', axis=1, ti...  10.7 us
    all_to_all x1, starting transfers between devices, on_device(): lax.all_to_all(part_cols.astype(jnp.bfloat16), 'seq', split_axis=0, conca...  6.43 us
  transfers between devices with their start and end apart: 4, of which 3 were waited for; matrix products, arithmetic and copies ran while one was open for 9% of the time, Pallas kernels for 0%

profile of v1, /device:TPU:13, one launch (start us, length us, event | category | flops | bytes accessed | tf_op | source)
XLA Modules:
  0.0 296.6 jit_solution(5290898509459888009)
XLA Ops:
  7.2 0.9 reshape.493
  8.9 0.8 reshape.494
  10.4 0.8 gather_fusion
  11.3 10.7 %all_gather.15 = bf16[48,8192]{1,0:T(8,128)(2,1)S(1)} all-gather(bf16[48,4096]{1,0:T(8,128)(2,1)S(1)} %select_select_fusion), channel_id=1, replica_groups=mesh['grp'=2,'seq'=16] {'grp'}, dimensions={1}, use_global_device_ids=true | all-gather | bytes 1179648 | tf_op jit(solution)/shard_map/all_gather | solution.py:82
  22.1 26.4 %all_to_all.50 = bf16[48,16,512]{2,0,1:T(8,128)(2,1)S(1)} all-to-all(bf16[48,16,512]{2,0,1:T(8,128)(2,1)S(1)} %bitcast.84), channel_id=1, replica_groups=mesh['grp'=2,'seq'=16] {'seq'}, dimensions={1} | all-to-all | bytes 1572864 | tf_op jit(solution)/shard_map/all_to_all | solution.py:85
  49.6 1.4 reshape.497
  51.0 2.7 convolution_convert_fusion.1
  53.7 49.2 %all_to_all.51 = bf16[16,48,1280]{2,1,0:T(8,128)(2,1)} all-to-all(bf16[16,48,1280]{2,1,0:T(8,128)(2,1)S(1)} %bitcast.85), channel_id=1, replica_groups=mesh['grp'=2,'seq'=16] {'seq'}, dimensions={0} | all-to-all | bytes 3932160 | tf_op jit(solution)/shard_map/all_to_all | solution.py:91
  103.0 1.9 reduce_sum.108
  104.9 0.8 fusion.26
  106.9 38.0 %all-gather.3.cloned.1.call-done = bf16[768,1280]{1,0:T(8,128)(2,1)} async-done(((bf16[48,1280]{1,0:T(8,128)(2,1)}), bf16[768,1280]{1,0:T(8,128)(2,1)}) %all-gather.3.cloned.1.call-update) | async-done | bytes 1966096 | tf_op jit(solution)/shard_map/all_gather | solution.py:99
  144.9 2.6 convolution_convert_fusion.2
  147.5 1.1 copy.22
  148.5 6.4 %all-to-all-start.2 = ((bf16[16,48,320]{2,1,0:T(8,128)(2,1)}), bf16[16,48,320]{2,1,0:T(8,128)(2,1)}, u32[]{:S(2)}, u32[]{:S(2)}) async-start(bf16[16,48,320]{2,1,0:T(8,128)(2,1)} %bitcast.13), calls=%async_computation.2 | async-start | bytes 1179648 | tf_op jit(solution)/shard_map/all_to_all | solution.py:101
  155.0 1.1 reshape.503
  156.6 20.1 %all-to-all-done.2 = bf16[16,48,320]{2,1,0:T(8,128)(2,1)} async-done(((bf16[16,48,320]{2,1,0:T(8,128)(2,1)}), bf16[16,48,320]{2,1,0:T(8,128)(2,1)}, u32[]{:S(2)}, u32[]{:S(2)}) %all-to-all-start.2) | async-done | bytes 491552 | tf_op jit(solution)/shard_map/all_to_all | solution.py:101
  176.7 2.0 copy.23
  178.7 2.3 all_gather.17
  181.0 13.6 %all_gather.18 = bf16[2,48,5120]{2,1,0:T(8,128)(2,1)S(1)} all-gather(bf16[1,48,5120]{2,1,0:T(8,128)(2,1)} %all_gather.17), channel_id=1, replica_groups=mesh['grp'=2,'seq'=16] {'grp'}, dimensions={0}, use_global_device_ids=true | all-gather | bytes 1474560 | tf_op jit(solution)/shard_map/all_gather | solution.py:105
  194.6 1.1 convert_reduce_fusion.1
  195.8 2.5 reshape.498
  198.3 2.4 multiply_reduce_fusion.1
  200.8 1.1 copy-done.1
  201.8 1.3 multiply_convert_fusion
  203.1 1.2 convert_element_type.82
  204.3 3.9 %convolution_convert_fusion = bf16[1280,1280]{1,0:T(8,128)(2,1)} fusion(bf16[192,1280]{1,0:T(8,128)(2,1)S(1)} %convert_element_type.82, bf16[192,1,1280]{2,0,1:T(8,128)(2,1)} %param.17), kind=kOutput, calls=%fused_computation.1 | convolution fusion | flops 632504320 | bytes 4259840 | tf_op jit(solution)/shard_map/dot_general | solution.py:135
  208.1 5.6 %all-to-all-start.3 = ((bf16[16,80,1280]{2,1,0:T(8,128)(2,1)}), bf16[16,80,1280]{2,1,0:T(8,128)(2,1)}, u32[]{:S(2)}, u32[]{:S(2)}) async-start(bf16[16,80,1280]{2,1,0:T(8,128)(2,1)} %bitcast.81), calls=%async_computation.3 | async-start | bytes 6553600 | tf_op jit(solution)/shard_map/all_to_all | solution.py:138
  213.9 1.1 reshape.499
  215.0 1.7 multiply_convert_fusion.1
  217.5 3.6 %fusion.1 = bf16[192,1,1280]{2,0,1:T(8,128)(2,1)} fusion(bf16[192,1280]{1,0:T(8,128)(2,1)S(1)} %multiply_convert_fusion.1, bf16[1280,1280]{1,0:T(8,128)(2,1)} %all-gather.5.cloned.1.call-done, bf16[192,1,1280]{2,0,1:T(8,128)(2,1)S(1)} %copy-done.6), kind=kOutput, calls=%fused_computation.6 | convolution fusion | flops 631848960 | bytes 4751360 | tf_op jit(solution)/shard_map/dot_general | solution.py:123
  221.1 65.5 %all-to-all-done.3 = bf16[16,80,1280]{2,1,0:T(8,128)(2,1)} async-done(((bf16[16,80,1280]{2,1,0:T(8,128)(2,1)}), bf16[16,80,1280]{2,1,0:T(8,128)(2,1)}, u32[]{:S(2)}, u32[]{:S(2)}) %all-to-all-start.3) | async-done | bytes 3276832 | tf_op jit(solution)/shard_map/all_to_all | solution.py:138
  286.6 3.2 %convert_reduce_fusion = f32[80,1280]{1,0:T(8,128)} fusion(bf16[16,80,1280]{2,1,0:T(8,128)(2,1)} %all-to-all-done.3), kind=kLoop, calls=%fused_computation.2 | loop fusion | flops 3174400 | bytes 3686400 | tf_op jit(solution)/shard_map/reduce_sum | solution.py:141
  (52 shorter events, 5.4 us)
Async XLA Ops:
  7.2 3.2 %copy-start = (bf16[256,4096]{1,0:T(8,128)(2,1)S(1)}, bf16[256,4096]{1,0:T(8,128)(2,1)}, u32[]{:S(2)}) copy-start(bf16[256,4096]{1,0:T(8,128)(2,1)} %param.11) | copy-start | bytes 6291460
  7.2 137.7 %all-gather.3.cloned.1.call-start = ((), (), s32[]{:S(2)}) async-start(), calls=%async_computation.4 | async-start | bytes 2088960 | tf_op jit(solution)/shard_map/all_gather | solution.py:99
  103.0 1.9 copy-start.4
  103.0 3.5 %copy-start.3 = (bf16[192,1,1280]{2,0,1:T(8,128)(2,1)S(1)}, bf16[192,1,1280]{2,0,1:T(8,128)(2,1)}, u32[]{:S(2)}) copy-start(bf16[192,1,1280]{2,0,1:T(8,128)(2,1)} %param.16) | copy-start | bytes 1474564
  105.7 111.8 %all-gather.5.cloned.1.call-start = ((), (), s32[]{:S(2)}) async-start(), calls=%async_computation.5 | async-start | bytes 3481600 | tf_op jit(solution)/shard_map/all_gather | solution.py:125
  148.5 28.2 %all-to-all-start.2 = ((bf16[16,48,320]{2,1,0:T(8,128)(2,1)}), bf16[16,48,320]{2,1,0:T(8,128)(2,1)}, u32[]{:S(2)}, u32[]{:S(2)}) async-start(bf16[16,48,320]{2,1,0:T(8,128)(2,1)} %bitcast.13), calls=%async_computation.2 | async-start | bytes 1179648 | tf_op jit(solution)/shard_map/all_to_all | solution.py:101
  195.8 2.6 copy-start.5
  200.7 1.1 copy-start.1
  208.1 5.7 %copy-start.2 = (f32[16,12,1280]{2,1,0:T(8,128)S(1)}, f32[16,12,1280]{2,1,0:T(8,128)}, u32[]{:S(2)}) copy-start(f32[16,12,1280]{2,1,0:T(8,128)} %copy-done.1) | copy-start | bytes 2949124
  208.1 78.4 %all-to-all-start.3 = ((bf16[16,80,1280]{2,1,0:T(8,128)(2,1)}), bf16[16,80,1280]{2,1,0:T(8,128)(2,1)}, u32[]{:S(2)}, u32[]{:S(2)}) async-start(bf16[16,80,1280]{2,1,0:T(8,128)(2,1)} %bitcast.81), calls=%async_computation.3 | async-start | bytes 6553600 | tf_op jit(solution)/shard_map/all_to_all | solution.py:138
  215.0 2.5 copy-start.6
Sparse Core Ops, SparseCore 0:
  105.8 39.0 all-gather.2
  147.2 52.0 all-gather.4
